TPU v7x, 8 devices: a whole 2x2x1 slice. The times are simulated.
8 devices in a mesh: prob: 2 (over z, y), feat: 4 (over x, core).
Axes of the slice: x: 2, y: 2, z: 1, core: 2. Of those that a mesh axis runs over, the one named last changes fastest.
Arguments:
- design: bfloat16 [16384, 16384], P(None, ('prob', 'feat')), parts along dimension 1
- w_init: float32 [16384, 101], P(('prob', 'feat')), parts along dimension 0
- targets: float32 [32768, 101], P('prob'), parts along dimension 0
Outputs:
- output 1: float32 [16384, 101], P(('prob', 'feat')), parts along dimension 0
- output 2: float32 [32768, 101], P('prob'), parts along dimension 0
There are 2 independent parts. A program takes and returns all parts, laid end to end along the dimension named above; each array names one.
All inputs are finite; a program needn't handle non-finite values.
Results may differ from a plain program's by a relative error of at most 0.0043035.
Values are sent between devices in bfloat16 or wider.
A program may use at most 1 GiB of HBM per device.

v0:
```python
import jax
import jax.numpy as jnp
from jax import lax
from jax.sharding import PartitionSpec as P

LOCAL_STEPS = 2
SWEEPS = 6
RIDGE = 0.01
GAMMA = 0.75


def block_product(x_block, coef_block):
    full = jnp.dot(x_block, coef_block.astype(jnp.bfloat16), preferred_element_type=jnp.float32)
    return full.astype(jnp.bfloat16).astype(jnp.float32)


def left_product(x_block, resid_part):
    return lax.dot_general(x_block, resid_part.astype(jnp.bfloat16), (((0,), (0,)), ((), ())), preferred_element_type=jnp.float32)


def solution(mesh):
    group_size = mesh.shape['feat']

    def per_device(design, w_init, targets):
        samples = design.shape[0]
        step_size = samples / (group_size * jnp.sum(jnp.square(design.astype(jnp.float32))))
        prediction = lax.psum(block_product(design, w_init), 'feat')
        residual = targets - prediction
        weights = w_init
        for sweep_idx in range(SWEEPS):
            gradient = left_product(design, residual) / samples
            coef_step = step_size * (gradient - RIDGE * weights)
            update = block_product(design, coef_step)
            for step_idx in range(1, LOCAL_STEPS):
                gradient = left_product(design, residual - group_size * update) / samples
                coef_step = coef_step + step_size * (gradient - RIDGE * (weights + coef_step))
                update = block_product(design, coef_step)
            residual = residual - GAMMA * lax.psum(update, 'feat')
            weights = weights + GAMMA * coef_step
        return weights, residual

    return jax.shard_map(
        per_device,
        mesh=mesh,
        in_specs=(P(None, ('prob', 'feat')), P(('prob', 'feat'), None), P('prob', None)),
        out_specs=(P(('prob', 'feat'), None), P('prob', None)),
        check_vma=False,
    )
```

profile of v0, /device:TPU:0, one launch (start us, length us, event | category | flops | bytes accessed | tf_op | source)
XLA Modules:
  0.0 1651.2 jit_solution(7903464661289018311)
XLA Ops:
  7.2 0.0 all-reduce.8.cloned.1.call-start
  7.2 31.3 %fusion.42 = f32[16384,101]{0,1:T(8,128)} fusion(bf16[16384,2048]{1,0:T(8,128)(2,1)} %param.3, f32[2048,101]{0,1:T(8,128)} %param.4), kind=kOutput, calls=%fused_computation.56 | convolution fusion | flops 6781511680 | bytes 74555392 | tf_op jit(solution)/shard_map/dot_general | solution.py:13
  38.5 0.0 all-reduce.8.cloned.1.call-update
  38.6 0.2 all-reduce.10.cloned.1.call-start
  38.8 37.0 %multiply_reduce_fusion = f32[]{:T(128)} fusion(bf16[16384,2048]{1,0:T(8,128)(2,1)} %param.3), kind=kLoop, calls=%fused_computation | loop fusion | flops 100663296 | bytes 67108864 | tf_op jit(solution)/shard_map/reduce_sum | solution.py:26
  76.5 0.0 copy-start
  76.5 87.4 %all-reduce.8.cloned.1.call-done = f32[16384,101]{0,1:T(8,128)} async-done(((f32[16384,101]{0,1:T(8,128)}), f32[16384,101]{0,1:T(8,128)}) %all-reduce.8.cloned.1.call-update) | async-done | bytes 6619152 | tf_op jit(solution)/shard_map/psum | solution.py:27
  163.9 8.5 sub.75
  172.4 0.0 copy-done
  172.4 24.9 %fusion.148 = f32[2048,101]{0,1:T(8,128)S(1)} fusion(bf16[16384,2048]{1,0:T(8,128)(2,1)} %param.3, f32[16384,101]{0,1:T(8,128)} %sub.75, f32[2048,101]{0,1:T(8,128)S(1)} %copy-done, f32[]{:T(128)S(6)} %div.63), kind=kOutput, calls=%fused_computation.122 | convolution fusion | flops 6780477440 | bytes 75382784 | tf_op jit(solution)/shard_map/dot_general | solution.py:18
  197.3 59.4 %fusion.168 = f32[2048,101]{0,1:T(8,128)S(1)} fusion(f32[2048,101]{0,1:T(8,128)S(1)} %fusion.148, bf16[16384,2048]{1,0:T(8,128)(2,1)} %param.3, f32[16384,101]{0,1:T(8,128)} %sub.75, f32[2048,101]{0,1:T(8,128)S(1)} %copy-done, f32[]{:T(128)S(6)} %div.63), kind=kOutput, calls=%fused_computation.140 | convolution fusion | flops 13565712384 | bytes 76210176 | tf_op jit(solution)/shard_map/dot_general | solution.py:18
  256.7 30.0 %fusion.6 = f32[16384,101]{0,1:T(8,128)} fusion(bf16[16384,2048]{1,0:T(8,128)(2,1)} %param.3, f32[2048,101]{0,1:T(8,128)S(1)} %fusion.168), kind=kOutput, calls=%fused_computation.19 | convolution fusion | flops 6781511680 | bytes 74555392 | tf_op jit(solution)/shard_map/dot_general | solution.py:13
  286.8 0.0 all-reduce.10.cloned.1.call-update
  286.8 0.3 all-reduce.12.cloned.1.call-start
  287.1 122.5 %all-reduce.10.cloned.1.call-done = f32[16384,101]{0,1:T(8,128)} async-done(((f32[16384,101]{0,1:T(8,128)}), f32[16384,101]{0,1:T(8,128)}) %all-reduce.10.cloned.1.call-update) | async-done | bytes 6619152 | tf_op jit(solution)/shard_map/psum | solution.py:38
  409.5 27.0 %fusion.142 = f32[2048,101]{0,1:T(8,128)S(1)} fusion(bf16[16384,2048]{1,0:T(8,128)(2,1)} %param.3, f32[]{:T(128)S(6)} %div.63, f32[2048,101]{0,1:T(8,128)S(1)} %copy-done, f32[2048,101]{0,1:T(8,128)S(1)} %fusion.168, f32[16384,101]{0,1:T(8,128)} %sub.75, f32[16384,101]{0,1:T(8,128)} %all-reduce.10.cloned.1.call-done), kind=kOutput, calls=%fused_computation.120 | convolution fusion | flops 6784200704 | bytes 82829312 | tf_op jit(solution)/shard_map/dot_general | solution.py:18
  436.5 63.0 %multiply_add_fusion.4 = (f32[2048,101]{0,1:T(8,128)S(1)}, bf16[2048,101]{0,1:T(8,128)(2,1)}) fusion(f32[2048,101]{0,1:T(8,128)S(1)} %copy-done, f32[2048,101]{0,1:T(8,128)S(1)} %fusion.168, f32[2048,101]{0,1:T(8,128)S(1)} %fusion.142, bf16[16384,2048]{1,0:T(8,128)(2,1)} %param.3, f32[16384,101]{0,1:T(8,128)} %sub.75, ...), kind=kOutput, calls=%fused_computation.145 | convolution fusion | flops 13570056192 | bytes 84070400 | tf_op jit(solution)/shard_map/dot_general | solution.py:18
  499.6 29.6 %fusion.13 = f32[16384,101]{0,1:T(8,128)} fusion(bf16[16384,2048]{1,0:T(8,128)(2,1)} %param.3, bf16[2048,101]{0,1:T(8,128)(2,1)} %get-tuple-element.3), kind=kOutput, calls=%fused_computation.26 | convolution fusion | flops 6781304832 | bytes 74141696 | tf_op jit(solution)/shard_map/dot_general | solution.py:13
  529.1 0.0 all-reduce.12.cloned.1.call-update
  529.1 0.4 all-reduce.14.cloned.1.call-start
  529.6 122.3 %all-reduce.12.cloned.1.call-done = f32[16384,101]{0,1:T(8,128)} async-done(((f32[16384,101]{0,1:T(8,128)}), f32[16384,101]{0,1:T(8,128)}) %all-reduce.12.cloned.1.call-update) | async-done | bytes 6619152 | tf_op jit(solution)/shard_map/psum | solution.py:38
  651.9 10.9 multiply_subtract_fusion.4
  662.8 24.9 %fusion.136 = f32[2048,101]{0,1:T(8,128)S(1)} fusion(bf16[16384,2048]{1,0:T(8,128)(2,1)} %param.3, f32[16384,101]{0,1:T(8,128)} %multiply_subtract_fusion.4, f32[2048,101]{0,1:T(8,128)S(1)} %get-tuple-element.2, f32[]{:T(128)S(6)} %div.63), kind=kOutput, calls=%fused_computation.118 | convolution fusion | flops 6780477440 | bytes 75382784 | tf_op jit(solution)/shard_map/dot_general | solution.py:18
  687.7 59.4 %fusion.162 = f32[2048,101]{0,1:T(8,128)S(1)} fusion(f32[2048,101]{0,1:T(8,128)S(1)} %fusion.136, bf16[16384,2048]{1,0:T(8,128)(2,1)} %param.3, f32[16384,101]{0,1:T(8,128)} %multiply_subtract_fusion.4, f32[2048,101]{0,1:T(8,128)S(1)} %get-tuple-element.2, f32[]{:T(128)S(6)} %div.63), kind=kOutput, calls=%fused_computation.134 | convolution fusion | flops 13565712384 | bytes 76210176 | tf_op jit(solution)/shard_map/dot_general | solution.py:18
  747.1 30.0 %fusion.20 = f32[16384,101]{0,1:T(8,128)} fusion(bf16[16384,2048]{1,0:T(8,128)(2,1)} %param.3, f32[2048,101]{0,1:T(8,128)S(1)} %fusion.162), kind=kOutput, calls=%fused_computation.33 | convolution fusion | flops 6781511680 | bytes 74555392 | tf_op jit(solution)/shard_map/dot_general | solution.py:13
  777.1 0.0 all-reduce.14.cloned.1.call-update
  777.2 0.2 all-reduce.16.cloned.1.call-start
  777.4 122.5 %all-reduce.14.cloned.1.call-done = f32[16384,101]{0,1:T(8,128)} async-done(((f32[16384,101]{0,1:T(8,128)}), f32[16384,101]{0,1:T(8,128)}) %all-reduce.14.cloned.1.call-update) | async-done | bytes 6619152 | tf_op jit(solution)/shard_map/psum | solution.py:38
  899.9 27.0 %fusion.130 = f32[2048,101]{0,1:T(8,128)S(1)} fusion(bf16[16384,2048]{1,0:T(8,128)(2,1)} %param.3, f32[]{:T(128)S(6)} %div.63, f32[2048,101]{0,1:T(8,128)S(1)} %get-tuple-element.2, f32[2048,101]{0,1:T(8,128)S(1)} %fusion.162, f32[16384,101]{0,1:T(8,128)} %multiply_subtract_fusion.4, f32[16384,101]{0,1:T(8,128)} %all-reduce.14.cloned.1.call-done), kind=kOutput, calls=%fused_computation.116 | convolution fusion | flops 6784200704 | bytes 82829312 | tf_op jit(solution)/shard_map/dot_general | solution.py:18
  926.9 63.0 %multiply_add_fusion.2 = (f32[2048,101]{0,1:T(8,128)S(1)}, bf16[2048,101]{0,1:T(8,128)(2,1)}) fusion(f32[2048,101]{0,1:T(8,128)S(1)} %get-tuple-element.2, f32[2048,101]{0,1:T(8,128)S(1)} %fusion.162, f32[2048,101]{0,1:T(8,128)S(1)} %fusion.130, bf16[16384,2048]{1,0:T(8,128)(2,1)} %param.3, f32[16384,101]{0,1:T(8,128)} %multiply_subtract_fusion.4, ...), kind=kOutput, calls=%fused_computation.143 | convolution fusion | flops 13570056192 | bytes 84070400 | tf_op jit(solution)/shard_map/dot_general | solution.py:18
  989.9 29.6 %fusion.27 = f32[16384,101]{0,1:T(8,128)} fusion(bf16[16384,2048]{1,0:T(8,128)(2,1)} %param.3, bf16[2048,101]{0,1:T(8,128)(2,1)} %get-tuple-element.5), kind=kOutput, calls=%fused_computation.40 | convolution fusion | flops 6781304832 | bytes 74141696 | tf_op jit(solution)/shard_map/dot_general | solution.py:13
  1019.5 0.0 all-reduce.16.cloned.1.call-update
  1019.5 0.3 all-reduce.18.cloned.1.call-start
  1019.8 122.5 %all-reduce.16.cloned.1.call-done = f32[16384,101]{0,1:T(8,128)} async-done(((f32[16384,101]{0,1:T(8,128)}), f32[16384,101]{0,1:T(8,128)}) %all-reduce.16.cloned.1.call-update) | async-done | bytes 6619152 | tf_op jit(solution)/shard_map/psum | solution.py:38
  1142.3 10.9 multiply_subtract_fusion.2
  1153.2 24.9 %fusion.124 = f32[2048,101]{0,1:T(8,128)S(1)} fusion(bf16[16384,2048]{1,0:T(8,128)(2,1)} %param.3, f32[16384,101]{0,1:T(8,128)} %multiply_subtract_fusion.2, f32[2048,101]{0,1:T(8,128)S(1)} %get-tuple-element.4, f32[]{:T(128)S(6)} %div.63), kind=kOutput, calls=%fused_computation.114 | convolution fusion | flops 6780477440 | bytes 75382784 | tf_op jit(solution)/shard_map/dot_general | solution.py:18
  1178.1 59.4 %fusion.156 = f32[2048,101]{0,1:T(8,128)S(1)} fusion(f32[2048,101]{0,1:T(8,128)S(1)} %fusion.124, bf16[16384,2048]{1,0:T(8,128)(2,1)} %param.3, f32[16384,101]{0,1:T(8,128)} %multiply_subtract_fusion.2, f32[2048,101]{0,1:T(8,128)S(1)} %get-tuple-element.4, f32[]{:T(128)S(6)} %div.63), kind=kOutput, calls=%fused_computation.128 | convolution fusion | flops 13565712384 | bytes 76210176 | tf_op jit(solution)/shard_map/dot_general | solution.py:18
  1237.5 30.0 %fusion.34 = f32[16384,101]{0,1:T(8,128)} fusion(bf16[16384,2048]{1,0:T(8,128)(2,1)} %param.3, f32[2048,101]{0,1:T(8,128)S(1)} %fusion.156), kind=kOutput, calls=%fused_computation.47 | convolution fusion | flops 6781511680 | bytes 74555392 | tf_op jit(solution)/shard_map/dot_general | solution.py:13
  1267.5 0.0 all-reduce.18.cloned.1.call-update
  1267.5 0.3 all-reduce.20.cloned.1.call-start
  1267.8 122.4 %all-reduce.18.cloned.1.call-done = f32[16384,101]{0,1:T(8,128)} async-done(((f32[16384,101]{0,1:T(8,128)}), f32[16384,101]{0,1:T(8,128)}) %all-reduce.18.cloned.1.call-update) | async-done | bytes 6619152 | tf_op jit(solution)/shard_map/psum | solution.py:38
  1390.3 27.0 %fusion.118 = f32[2048,101]{0,1:T(8,128)S(1)} fusion(bf16[16384,2048]{1,0:T(8,128)(2,1)} %param.3, f32[]{:T(128)S(6)} %div.63, f32[2048,101]{0,1:T(8,128)S(1)} %get-tuple-element.4, f32[2048,101]{0,1:T(8,128)S(1)} %fusion.156, f32[16384,101]{0,1:T(8,128)} %multiply_subtract_fusion.2, f32[16384,101]{0,1:T(8,128)} %all-reduce.18.cloned.1.call-done), kind=kOutput, calls=%fused_computation.112 | convolution fusion | flops 6784200704 | bytes 82829312 | tf_op jit(solution)/shard_map/dot_general | solution.py:18
  1417.3 63.2 %multiply_add_fusion = (f32[2048,101]{0,1:T(8,128)}, bf16[2048,101]{0,1:T(8,128)(2,1)S(1)}) fusion(f32[2048,101]{0,1:T(8,128)S(1)} %get-tuple-element.4, f32[2048,101]{0,1:T(8,128)S(1)} %fusion.156, f32[2048,101]{0,1:T(8,128)S(1)} %fusion.118, bf16[16384,2048]{1,0:T(8,128)(2,1)} %param.3, f32[16384,101]{0,1:T(8,128)} %multiply_subtract_fusion.2, ...), kind=kOutput, calls=%fused_computation.141 | convolution fusion | flops 13570056192 | bytes 84070400 | tf_op jit(solution)/shard_map/dot_general | solution.py:18
  1480.5 30.0 %fusion.41 = f32[16384,101]{0,1:T(8,128)} fusion(bf16[16384,2048]{1,0:T(8,128)(2,1)} %param.3, bf16[2048,101]{0,1:T(8,128)(2,1)S(1)} %get-tuple-element.7), kind=kOutput, calls=%fused_computation.54 | convolution fusion | flops 6781304832 | bytes 74141696 | tf_op jit(solution)/shard_map/dot_general | solution.py:13
  1510.5 0.0 all-reduce.20.cloned.1.call-update
  1510.5 122.7 %all-reduce.20.cloned.1.call-done = f32[16384,101]{0,1:T(8,128)} async-done(((f32[16384,101]{0,1:T(8,128)}), f32[16384,101]{0,1:T(8,128)}) %all-reduce.20.cloned.1.call-update) | async-done | bytes 6619152 | tf_op jit(solution)/shard_map/psum | solution.py:38
  1633.2 10.9 multiply_subtract_fusion
Async XLA Ops:
  7.2 156.7 %all-reduce.8.cloned.1.call-start = ((), (), s32[]{:S(2)}) async-start(), calls=%async_computation | async-start | bytes 13631488 | tf_op jit(solution)/shard_map/psum | solution.py:27
  38.6 371.0 %all-reduce.10.cloned.1.call-start = ((), (), s32[]{:S(2)}) async-start(), calls=%async_computation.1 | async-start | bytes 13631488 | tf_op jit(solution)/shard_map/psum | solution.py:38
  76.5 95.9 %copy-start = (f32[2048,101]{0,1:T(8,128)S(1)}, f32[2048,101]{0,1:T(8,128)}, u32[]{:S(2)}) copy-start(f32[2048,101]{0,1:T(8,128)} %param.4) | copy-start | bytes 2482180
  286.8 365.1 %all-reduce.12.cloned.1.call-start = ((), (), s32[]{:S(2)}) async-start(), calls=%async_computation.2 | async-start | bytes 13631488 | tf_op jit(solution)/shard_map/psum | solution.py:38
  529.1 370.8 %all-reduce.14.cloned.1.call-start = ((), (), s32[]{:S(2)}) async-start(), calls=%async_computation.3 | async-start | bytes 13631488 | tf_op jit(solution)/shard_map/psum | solution.py:38
  777.2 365.1 %all-reduce.16.cloned.1.call-start = ((), (), s32[]{:S(2)}) async-start(), calls=%async_computation.4 | async-start | bytes 13631488 | tf_op jit(solution)/shard_map/psum | solution.py:38
  1019.5 370.7 %all-reduce.18.cloned.1.call-start = ((), (), s32[]{:S(2)}) async-start(), calls=%async_computation.5 | async-start | bytes 13631488 | tf_op jit(solution)/shard_map/psum | solution.py:38
  1267.5 365.7 %all-reduce.20.cloned.1.call-start = ((), (), s32[]{:S(2)}) async-start(), calls=%async_computation.6 | async-start | bytes 13631488 | tf_op jit(solution)/shard_map/psum | solution.py:38
Sparse Core Ops, SparseCore 0:
  38.7 125.1 all-reduce.7
  286.9 122.5 all-reduce.9
  529.3 122.5 all-reduce.11
  777.3 122.5 all-reduce.13
  1019.7 122.5 all-reduce.15
  1267.6 122.5 all-reduce.17
  1510.6 122.5 all-reduce.19
where the time goes:
time: 1660 us; the launch traced here: 1650 us
  waiting for transfers between devices  822 us (50%)
  matrix products  734 us (44%)
  other arithmetic  78.2 us (5%)
    psum x6, waiting for transfers between devices, per_device(): residual = residual - GAMMA * lax.psum(update, 'feat')  735 us
    dot_general x12, matrix products, left_product(): lax.dot_general(x_block, resid_part.astype(jnp.bfloat16), (((0,), (0,)),...  523 us
    dot_general x7, matrix products, block_product(): jnp.dot(x_block, coef_block.astype(jnp.bfloat16), preferred_element_type=...  211 us
    psum x1, waiting for transfers between devices, per_device(): prediction = lax.psum(block_product(design, w_init), 'feat')  87.4 us
    reduce_sum x1, other arithmetic, per_device(): jnp.sum(jnp.square(design.astype(jnp.float32)))  37 us
  transfers between devices with their start and end apart: 7, of which 7 were waited for; matrix products, arithmetic and copies ran while one was open for 2% of the time, Pallas kernels for 0%

commit v1 on v0

v1 whole, which is shorter than its diff:
```python
import functools

import jax
import jax.numpy as jnp
from jax import lax
from jax.experimental import pallas as pl
from jax.experimental.pallas import tpu as pltpu
from jax.sharding import PartitionSpec as P

LOCAL_STEPS = 2
SWEEPS = 6
RIDGE = 0.01
GAMMA = 0.75

MESH = pl.DeviceIdType.MESH
F32 = jnp.float32
BF16 = jnp.bfloat16
ROWS = 104
CHUNK = 512
RING = 8
BLOCK = 512
SIB, CROSS, DIAG = 0, 1, 2


def dot(a, b, dims=((1,), (0,))):
    return lax.dot_general(a, b, (dims, ((), ())), preferred_element_type=F32)


def kernel(samples, group, x_hbm, w0_ref, y_ref, w_ref, r_hbm,
           xbuf, xt, gram, gram_hi, gram_lo, eta_ref, coef, grad, r_own, r_all, u_mine, u_out, u_in,
           x_sem, u_send, u_recv, r_send, r_recv, o_send, o_recv, o_local):
    prob, me = lax.axis_index("prob"), lax.axis_index("feat")
    odd, half = lax.rem(me, 2), me // 2
    sib = half * 2 + (1 - odd)
    cross = (1 - half) * 2 + odd
    diag = (1 - half) * 2 + (1 - odd)
    partner = {SIB: sib, CROSS: cross, DIAG: diag}
    features = x_hbm.shape[1]
    quarter = samples // group
    steps = quarter // CHUNK
    blocks = features // BLOCK

    def device(index):
        return dict(device_id=(prob, index), device_id_type=MESH)

    barrier = pltpu.get_barrier_semaphore()
    for index in (sib, cross, diag):
        pl.semaphore_signal(barrier, inc=1, **device(index))

    def cols(c):
        return pl.ds(pl.multiple_of(c * CHUNK, CHUNK), CHUNK)

    def load(q, c, slot):
        rows = pl.ds(pl.multiple_of(q * quarter + c * CHUNK, CHUNK), CHUNK)
        return pltpu.make_async_copy(x_hbm.at[rows], xbuf.at[slot], x_sem.at[slot])

    a_order = (cross, diag, sib, me)
    b_order = (me, sib)
    c_order = (cross, diag)
    per = {"a": RING // 4, "b": RING // 2, "c": RING // 2}
    orders = {"a": a_order, "b": b_order, "c": c_order}

    def prefetch(phase, c, i, slot):
        if phase == "gram":
            load(0, c, slot).start()
        elif phase is not None:
            load(orders[phase][i], c, slot).start()

    def rounds(phase, nxt, body):
        n, order = per[phase], orders[phase]
        width = len(order)

        def run(c, ahead):
            for i in range(width):
                slot = lax.rem(c * width + i, RING)
                load(order[i], c, slot).wait()
                body(c, i, order[i], xbuf.at[slot])
                ahead(c, i, slot)

        def main(c, carry):
            run(c, lambda c, i, slot: prefetch(phase, c + n, i, slot))
            return carry

        def tail(c, carry):
            def ahead(c, i, slot):
                if nxt is None:
                    return
                k = (c - (steps - n)) * width + i
                if nxt == "gram":
                    prefetch(nxt, k, 0, slot)
                elif len(orders[nxt]) == width:
                    prefetch(nxt, c - (steps - n), i, slot)
                elif width == 4:
                    prefetch(nxt, (c - (steps - n)) * 2 + i // 2, i % 2, slot)
                else:
                    j = lax.rem(c - (steps - n), 2)
                    lo, hi = orders[nxt][i], orders[nxt][2 + i]
                    load(lo + j * (hi - lo), (c - (steps - n)) // 2, slot).start()
            run(c, ahead)
            return carry

        lax.fori_loop(0, steps - n, main, 0)
        lax.fori_loop(steps - n, steps, tail, 0)

    def u_copy(rel, c):
        return pltpu.make_async_remote_copy(
            u_out.at[rel, :, cols(c)], u_in.at[rel, :, cols(c)],
            u_send.at[rel, c], u_recv.at[rel, c], **device(partner[rel]))

    def r_copy(rel, c, q, target):
        return pltpu.make_async_remote_copy(
            r_all.at[q, :, cols(c)], r_all.at[q, :, cols(c)],
            r_send.at[rel, c], r_recv.at[rel, c], **device(target))

    a_rel = (CROSS, DIAG, SIB, None)

    def phase_a(nxt):
        def body(c, i, q, x):
            u = dot(coef[...], x[...], ((1,), (1,))).astype(BF16)
            if a_rel[i] is None:
                u_mine[:, cols(c)] = u
            else:
                u_out[a_rel[i], :, cols(c)] = u
                u_copy(a_rel[i], c).start()
        rounds("a", nxt, body)

    def residual(c, factor):
        for rel in (SIB, CROSS, DIAG):
            u_copy(rel, c).wait_recv()
        total = u_mine[:, cols(c)].astype(F32)
        for rel in (SIB, CROSS, DIAG):
            total = total + u_in[rel, :, cols(c)].astype(F32)
        new = r_own[:, cols(c)] - factor * total
        r_own[:, cols(c)] = new
        return new

    def update(c, factor):
        r_all[me, :, cols(c)] = residual(c, factor).astype(BF16)
        r_copy(CROSS, c, me, cross).start()
        r_copy(SIB, c, me, sib).start()

    def accumulate(c, q, x):
        grad[...] += dot(r_all[q, :, cols(c)], x[...])

    def phase_b(factor):
        def body(c, i, q, x):
            if i == 0:
                if factor is not None:
                    update(c, factor)
            else:
                r_copy(SIB, c, sib, sib).wait_recv()
            accumulate(c, q, x)
        grad[...] = jnp.zeros_like(grad)
        rounds("b", "c", body)

    def phase_c():
        def body(c, i, q, x):
            if i == 0:
                r_copy(CROSS, c, cross, cross).wait_recv()
                r_copy(DIAG, c, cross, sib).start()
            else:
                r_copy(DIAG, c, diag, sib).wait_recv()
            accumulate(c, q, x)
        rounds("c", "a", body)

    def wait_u(c, carry):
        for rel in (SIB, CROSS, DIAG):
            u_copy(rel, c).wait_send()
        return carry

    def wait_r(c, carry):
        r_copy(CROSS, c, me, cross).wait_send()
        r_copy(SIB, c, me, sib).wait_send()
        r_copy(DIAG, c, cross, sib).wait_send()
        return carry

    def local_passes():
        eta = eta_ref[...]
        weights = w_ref[...]
        first = eta * (grad[...] * (1.0 / samples) - RIDGE * weights)
        lhs = first.astype(BF16)
        curved = dot(lhs, gram_hi[...]) + dot(lhs, gram_lo[...])
        curved = jnp.where(eta > 0, curved, 0.0)
        gradient = (grad[...] - (4.0 * group) * curved) * (1.0 / samples)
        second = first + eta * (gradient - RIDGE * (weights + first))
        w_ref[...] = weights + GAMMA * second
        coef[...] = second.astype(BF16)

    def block_index(i, j):
        return i * (i + 1) // 2 + j

    def gram_steps(start, stop, ahead):
        def step(k, carry):
            slot = lax.rem(k, RING)
            load(0, k, slot).wait()
            xt[...] = xbuf[slot].T
            for i in range(blocks):
                for j in range(i + 1):
                    left = xt[i * BLOCK:(i + 1) * BLOCK, :]
                    right = xbuf[slot, :, j * BLOCK:(j + 1) * BLOCK]
                    gram[block_index(i, j)] += dot(left, right)
            ahead(k, slot)
            return carry
        lax.fori_loop(start, stop, step, 0)

    def gram_finish():
        trace = jnp.zeros((1, 1), F32)
        for i in range(blocks):
            for j in range(i + 1):
                block = gram[block_index(i, j)]
                if i == j:
                    row = lax.broadcasted_iota(jnp.int32, block.shape, 0)
                    col = lax.broadcasted_iota(jnp.int32, block.shape, 1)
                    picked = jnp.where(row == col, block, 0.0)
                    trace = trace + jnp.sum(jnp.sum(picked, axis=0, keepdims=True), axis=1, keepdims=True)
                scaled = block * 0.25
                rows, columns = slice(i * BLOCK, (i + 1) * BLOCK), slice(j * BLOCK, (j + 1) * BLOCK)
                high = scaled.astype(BF16)
                gram_hi[rows, columns] = high
                gram_lo[rows, columns] = (scaled - high.astype(F32)).astype(BF16)
                if i != j:
                    scaled = scaled.T
                    high = scaled.astype(BF16)
                    gram_hi[columns, rows] = high
                    gram_lo[columns, rows] = (scaled - high.astype(F32)).astype(BF16)
        eta_ref[...] = jnp.broadcast_to(samples / (group * trace), eta_ref.shape)

    for k in range(RING):
        load(a_order[k % 4], k // 4, k).start()
    coef[...] = w0_ref[...].astype(BF16)
    w_ref[...] = w0_ref[...]
    r_own[...] = y_ref[...]
    gram[...] = jnp.zeros_like(gram)
    pl.semaphore_wait(barrier, 3)
    phase_a("gram")
    total_steps = samples // CHUNK
    gram_steps(0, total_steps // 2, lambda k, slot: load(0, k + RING, slot).start())

    def first_update(c, carry):
        update(c, 1.0)
        return carry

    lax.fori_loop(0, steps, first_update, 0)
    gram_steps(total_steps // 2, total_steps - RING, lambda k, slot: load(0, k + RING, slot).start())

    def to_b(k, slot):
        j = k - (total_steps - RING)
        load(me + lax.rem(j, 2) * (sib - me), j // 2, slot).start()

    gram_steps(total_steps - RING, total_steps, to_b)
    gram_finish()
    lax.fori_loop(0, steps, wait_u, 0)
    phase_b(None)
    phase_c()
    lax.fori_loop(0, steps, wait_r, 0)
    local_passes()

    def sweep(t, carry):
        phase_a("b")
        phase_b(GAMMA)
        phase_c()
        lax.fori_loop(0, steps, wait_u, 0)
        lax.fori_loop(0, steps, wait_r, 0)
        local_passes()
        return carry

    lax.fori_loop(0, SWEEPS - 1, sweep, 0)

    phase_a(None)

    def o_copy(rel, c, q, target, source):
        return pltpu.make_async_remote_copy(
            source, r_hbm.at[q, :, cols(c)], o_send.at[rel, c], o_recv.at[rel, c], **device(target))

    def o_keep(c):
        return pltpu.make_async_copy(r_own.at[:, cols(c)], r_hbm.at[me, :, cols(c)], o_local.at[c])

    def finish(c, carry):
        residual(c, GAMMA)
        o_copy(CROSS, c, me, cross, r_own.at[:, cols(c)]).start()
        o_copy(SIB, c, me, sib, r_own.at[:, cols(c)]).start()
        o_keep(c).start()
        return carry

    def relay(c, carry):
        o_copy(CROSS, c, cross, cross, r_own.at[:, cols(c)]).wait_recv()
        o_copy(DIAG, c, cross, sib, r_hbm.at[cross, :, cols(c)]).start()
        return carry

    def drain(c, carry):
        o_copy(SIB, c, sib, sib, r_own.at[:, cols(c)]).wait_recv()
        o_copy(DIAG, c, diag, sib, r_own.at[:, cols(c)]).wait_recv()
        for rel, target in ((CROSS, cross), (SIB, sib)):
            o_copy(rel, c, me, target, r_own.at[:, cols(c)]).wait_send()
        o_copy(DIAG, c, cross, sib, r_hbm.at[cross, :, cols(c)]).wait_send()
        o_keep(c).wait()
        return carry

    lax.fori_loop(0, steps, finish, 0)
    lax.fori_loop(0, steps, relay, 0)
    lax.fori_loop(0, steps, wait_u, 0)
    lax.fori_loop(0, steps, drain, 0)


def solution(mesh):
    group = mesh.shape['feat']

    def per_device(design, w_init, targets):
        samples, features = design.shape
        labels = w_init.shape[1]
        quarter = samples // group
        steps = quarter // CHUNK
        blocks = features // BLOCK
        pad = ((0, ROWS - labels), (0, 0))
        own = lax.dynamic_slice_in_dim(targets, lax.axis_index('feat') * quarter, quarter, 0)
        w_t = jnp.pad(w_init.T, pad)
        y_t = jnp.pad(own.T, pad)
        vmem = pl.BlockSpec(memory_space=pltpu.VMEM)
        anywhere = pl.BlockSpec(memory_space=pl.ANY)
        dma = pltpu.SemaphoreType.DMA
        weights, residual = pl.pallas_call(
            functools.partial(kernel, samples, group),
            out_shape=(jax.ShapeDtypeStruct((ROWS, features), F32),
                       jax.ShapeDtypeStruct((group, ROWS, quarter), F32)),
            in_specs=[anywhere, vmem, vmem],
            out_specs=(vmem, anywhere),
            scratch_shapes=[
                pltpu.VMEM((RING, CHUNK, features), BF16),
                pltpu.VMEM((features, CHUNK), BF16),
                pltpu.VMEM((blocks * (blocks + 1) // 2, BLOCK, BLOCK), F32),
                pltpu.VMEM((features, features), BF16),
                pltpu.VMEM((features, features), BF16),
                pltpu.VMEM((1, features), F32),
                pltpu.VMEM((ROWS, features), BF16),
                pltpu.VMEM((ROWS, features), F32),
                pltpu.VMEM((ROWS, quarter), F32),
                pltpu.VMEM((group, ROWS, quarter), BF16),
                pltpu.VMEM((ROWS, quarter), BF16),
                pltpu.VMEM((3, ROWS, quarter), BF16),
                pltpu.VMEM((3, ROWS, quarter), BF16),
                dma((RING,)),
                dma((3, steps)), dma((3, steps)),
                dma((3, steps)), dma((3, steps)),
                dma((3, steps)), dma((3, steps)),
                dma((steps,)),
            ],
            compiler_params=pltpu.CompilerParams(
                collective_id=0, has_side_effects=True, vmem_limit_bytes=67000000),
        )(design, w_t, y_t)
        residual = residual.transpose(0, 2, 1).reshape(samples, ROWS)[:, :labels]
        return weights.T[:, :labels], residual

    return jax.shard_map(
        per_device,
        mesh=mesh,
        in_specs=(P(None, ('prob', 'feat')), P(('prob', 'feat'), None), P('prob', None)),
        out_specs=(P(('prob', 'feat'), None), P('prob', None)),
        check_vma=False,
    )
```

time: 1660 us -> 555 us (0.33)
  waiting for transfers between devices: 822 us -> 0 us
  matrix products: 734 us -> 0 us
  Pallas kernels: 0 us -> 541 us
  other arithmetic: 78.2 us -> 0 us
    psum x7 -> x0, waiting for transfers between devices: 822 us -> none  [the longest x6 735 us: per_device(): residual = residual - GAMMA * lax.psum(update, 'feat')]
    dot_general x19 -> x0, matrix products: 734 us -> none  [the longest x12 523 us: left_product(): lax.dot_general(x_block, resid_part.astype(jnp.bfloat16), (((0,), (0,)),...]
    pallas_call x0 -> x1, Pallas kernels: none -> 541 us  [per_device(): pl.pallas_call(functools.partial(kernel, samples, group), out_shape=(jax....]
    sub x4 -> x0, other arithmetic: 41.1 us -> none  [the longest x3 32.6 us: per_device(): residual = residual - GAMMA * lax.psum(update, 'feat')]
    reduce_sum x1 -> x0, other arithmetic: 37 us -> none  [per_device(): jnp.sum(jnp.square(design.astype(jnp.float32)))]
  transfers between devices with their start and end apart: 7 -> 0, of which waited for: 7 -> 0; matrix products, arithmetic and copies ran while one was open for 2% -> 0% of each run, Pallas kernels for 0% -> 0%
where the time goes in v1:
time: 555 us; the launch traced here: 554 us
  Pallas kernels  541 us (97%)
  local copies, waits for them, and re-layouts  12.6 us (2%)
    pallas_call x1, Pallas kernels, per_device(): pl.pallas_call(functools.partial(kernel, samples, group), out_shape=(jax....  541 us

profile of v1, /device:TPU:0, one launch (start us, length us, event | category | flops | bytes accessed | tf_op | source)
XLA Modules:
  0.0 554.4 jit_solution(11723748816816229365)
XLA Ops:
  0.6 2.1 pad.8.w0_ref
  2.8 1.6 dynamic-slice_bitcast_fusion
  4.3 1.3 pad.9.y_ref
  5.7 541.1 %shard_map.50 = (f32[104,2048]{1,0:T(8,128)}, f32[4,104,4096]{2,1,0:T(8,128)}) custom-call(bf16[16384,2048]{1,0:T(8,128)(2,1)} %x_hbm.1, f32[104,2048]{1,0:T(8,128)} %pad.8.w0_ref, f32[104,4096]{1,0:T(8,128)} %pad.9.y_ref), custom_call_target="tpu_custom_call" | custom-call | tf_op jit(solution)/shard_map/pallas_call | solution.py:321
  546.8 0.0 copy-start
  546.8 6.7 %copy.6 = f32[4,13,8,4096]{3,2,0,1:T(8,128)} copy(f32[4,13,8,4096]{3,2,1,0:T(8,128)} %bitcast.10) | data formatting | bytes 13631488 | tf_op jit(solution)/shard_map/reshape | solution.py:350
  553.5 0.0 copy-done
  553.5 0.9 copy.8
Async XLA Ops:
  546.8 6.7 %copy-start = (f32[104,2048]{1,0:T(8,128)S(1)}, f32[104,2048]{1,0:T(8,128)}, u32[]{:S(2)}) copy-start(f32[104,2048]{1,0:T(8,128)} %get-tuple-element.4) | copy-start | bytes 2555908

commit v2 on v1

--- a/solution.py
+++ b/solution.py
@@ -15,10 +15,10 @@
 MESH = pl.DeviceIdType.MESH
 F32 = jnp.float32
 BF16 = jnp.bfloat16
-ROWS = 104
 CHUNK = 512
 RING = 8
 BLOCK = 512
+HALF = BLOCK // 2
 SIB, CROSS, DIAG = 0, 1, 2
 
 
@@ -26,9 +26,9 @@
     return lax.dot_general(a, b, (dims, ((), ())), preferred_element_type=F32)
 
 
-def kernel(samples, group, x_hbm, w0_ref, y_ref, w_ref, r_hbm,
-           xbuf, xt, gram, gram_hi, gram_lo, eta_ref, coef, grad, r_own, r_all, u_mine, u_out, u_in,
-           x_sem, u_send, u_recv, r_send, r_recv, o_send, o_recv, o_local):
+def kernel(samples, group, x_hbm, w0_hbm, y_hbm, w_ref, r_hbm,
+           xbuf, xt0, xt1, gram, gram_hi, gram_lo, eta_ref, coef, grad, r_own, r_all, u_mine, u_out, u_in,
+           x_sem, u_send, u_recv, r_send, r_recv, o_send, o_recv, o_local, in_sem):
     prob, me = lax.axis_index("prob"), lax.axis_index("feat")
     odd, half = lax.rem(me, 2), me // 2
     sib = half * 2 + (1 - odd)
@@ -61,21 +61,23 @@
     orders = {"a": a_order, "b": b_order, "c": c_order}
 
     def prefetch(phase, c, i, slot):
-        if phase == "gram":
-            load(0, c, slot).start()
-        elif phase is not None:
-            load(orders[phase][i], c, slot).start()
-
-    def rounds(phase, nxt, body):
+        load(orders[phase][i], c, slot).start()
+
+    def rounds(phase, nxt, body, together=1):
         n, order = per[phase], orders[phase]
         width = len(order)
 
         def run(c, ahead):
-            for i in range(width):
-                slot = lax.rem(c * width + i, RING)
-                load(order[i], c, slot).wait()
-                body(c, i, order[i], xbuf.at[slot])
-                ahead(c, i, slot)
+            for first in range(0, width, together):
+                some = range(first, first + together)
+                slots = [lax.rem(c * width + i, RING) for i in some]
+                for i, slot in zip(some, slots):
+                    load(order[i], c, slot).wait()
+                sends = [body(c, i, order[i], xbuf.at[slot]) for i, slot in zip(some, slots)]
+                for i, slot, send in zip(some, slots, sends):
+                    if send is not None:
+                        send.start()
+                    ahead(c, i, slot)
 
         def main(c, carry):
             run(c, lambda c, i, slot: prefetch(phase, c + n, i, slot))
@@ -86,8 +88,8 @@
                 if nxt is None:
                     return
                 k = (c - (steps - n)) * width + i
-                if nxt == "gram":
-                    prefetch(nxt, k, 0, slot)
+                if nxt == "start":
+                    load(diag, k, slot).start()
                 elif len(orders[nxt]) == width:
                     prefetch(nxt, c - (steps - n), i, slot)
                 elif width == 4:
@@ -114,15 +116,15 @@
 
     a_rel = (CROSS, DIAG, SIB, None)
 
-    def phase_a(nxt):
+    def phase_a(nxt, together=1):
         def body(c, i, q, x):
             u = dot(coef[...], x[...], ((1,), (1,))).astype(BF16)
             if a_rel[i] is None:
                 u_mine[:, cols(c)] = u
-            else:
-                u_out[a_rel[i], :, cols(c)] = u
-                u_copy(a_rel[i], c).start()
-        rounds("a", nxt, body)
+                return None
+            u_out[a_rel[i], :, cols(c)] = u
+            return u_copy(a_rel[i], c)
+        rounds("a", nxt, body, together)
 
     def residual(c, factor):
         for rel in (SIB, CROSS, DIAG):
@@ -142,11 +144,10 @@
     def accumulate(c, q, x):
         grad[...] += dot(r_all[q, :, cols(c)], x[...])
 
-    def phase_b(factor):
+    def phase_b():
         def body(c, i, q, x):
             if i == 0:
-                if factor is not None:
-                    update(c, factor)
+                update(c, GAMMA)
             else:
                 r_copy(SIB, c, sib, sib).wait_recv()
             accumulate(c, q, x)
@@ -171,6 +172,9 @@
     def wait_r(c, carry):
         r_copy(CROSS, c, me, cross).wait_send()
         r_copy(SIB, c, me, sib).wait_send()
+        return carry
+
+    def wait_relay(c, carry):
         r_copy(DIAG, c, cross, sib).wait_send()
         return carry
 
@@ -189,19 +193,49 @@
     def block_index(i, j):
         return i * (i + 1) // 2 + j
 
-    def gram_steps(start, stop, ahead):
-        def step(k, carry):
-            slot = lax.rem(k, RING)
-            load(0, k, slot).wait()
-            xt[...] = xbuf[slot].T
-            for i in range(blocks):
-                for j in range(i + 1):
-                    left = xt[i * BLOCK:(i + 1) * BLOCK, :]
-                    right = xbuf[slot, :, j * BLOCK:(j + 1) * BLOCK]
+    def gram_add(left_ref, right_ref):
+        for i in range(blocks):
+            for j in range(i + 1):
+                left = left_ref[i * BLOCK:(i + 1) * BLOCK, :]
+                right = right_ref[:, j * BLOCK:(j + 1) * BLOCK]
+                if i == j:
+                    gram[block_index(i, j), HALF:, :] += dot(left[HALF:], right)
+                    gram[block_index(i, j), :HALF, :HALF] += dot(left[:HALF], right[:, :HALF])
+                else:
                     gram[block_index(i, j)] += dot(left, right)
-            ahead(k, slot)
+
+    def start_order(s):
+        flip_half, flip_odd = lax.rem(1 + (s + 1) // 2, 2), lax.rem(s + 1, 2)
+        return 2 * (half + flip_half * (1 - 2 * half)) + odd + flip_odd * (1 - 2 * odd)
+
+    def start_quarters(first, last, with_gradient):
+        def pair(t, carry):
+            s, k = t // (steps // 2), lax.rem(t, steps // 2)
+            q = start_order(s)
+            pairs = ((xt0, xt1), (xt1, xt0))
+            for i in range(2):
+                c = 2 * k + i
+                ahead = lax.rem(c + 1, RING)
+                load(q, ahead, ahead).wait()
+                if with_gradient:
+                    @pl.when(s == 2)
+                    def _():
+                        r_copy(SIB, c, sib, sib).wait_recv()
+
+                    @pl.when(s == 3)
+                    def _():
+                        r_copy(CROSS, c, cross, cross).wait_recv()
+                        r_copy(DIAG, c, cross, sib).start()
+            for i, (now, later) in enumerate(pairs):
+                c = 2 * k + i
+                later[...] = xbuf[lax.rem(c + 1, RING)].T
+                gram_add(now, xbuf.at[c])
+                if with_gradient:
+                    accumulate(c, q, xbuf.at[c])
+            for i in range(2):
+                load(start_order(s + 1), 2 * k + i, 2 * k + i).start()
             return carry
-        lax.fori_loop(start, stop, step, 0)
+        lax.fori_loop(first * (steps // 2), last * (steps // 2), pair, 0)
 
     def gram_finish():
         trace = jnp.zeros((1, 1), F32)
@@ -209,6 +243,8 @@
             for j in range(i + 1):
                 block = gram[block_index(i, j)]
                 if i == j:
+                    corner = jnp.concatenate([block[:HALF, :HALF], block[HALF:, :HALF].T], axis=1)
+                    block = jnp.concatenate([corner, block[HALF:]], axis=0)
                     row = lax.broadcasted_iota(jnp.int32, block.shape, 0)
                     col = lax.broadcasted_iota(jnp.int32, block.shape, 1)
                     picked = jnp.where(row == col, block, 0.0)
@@ -225,55 +261,71 @@
                     gram_lo[columns, rows] = (scaled - high.astype(F32)).astype(BF16)
         eta_ref[...] = jnp.broadcast_to(samples / (group * trace), eta_ref.shape)
 
+    in_w = pltpu.make_async_copy(w0_hbm, w_ref, in_sem.at[0])
+    in_y = pltpu.make_async_copy(
+        y_hbm.at[:, pl.ds(pl.multiple_of(me * quarter, quarter), quarter)], r_own, in_sem.at[1])
+    in_w.start()
     for k in range(RING):
         load(a_order[k % 4], k // 4, k).start()
-    coef[...] = w0_ref[...].astype(BF16)
-    w_ref[...] = w0_ref[...]
-    r_own[...] = y_ref[...]
+    in_y.start()
+    in_w.wait()
+    coef[...] = w_ref[...].astype(BF16)
+    pl.semaphore_wait(barrier, 3)
+    phase_a("start", 2)
     gram[...] = jnp.zeros_like(gram)
-    pl.semaphore_wait(barrier, 3)
-    phase_a("gram")
-    total_steps = samples // CHUNK
-    gram_steps(0, total_steps // 2, lambda k, slot: load(0, k + RING, slot).start())
+    grad[...] = jnp.zeros_like(grad)
+    in_y.wait()
 
     def first_update(c, carry):
         update(c, 1.0)
         return carry
 
+    load(diag, 0, 0).wait()
+    xt0[...] = xbuf[0].T
+    start_quarters(0, 1, False)
     lax.fori_loop(0, steps, first_update, 0)
-    gram_steps(total_steps // 2, total_steps - RING, lambda k, slot: load(0, k + RING, slot).start())
-
-    def to_b(k, slot):
-        j = k - (total_steps - RING)
-        load(me + lax.rem(j, 2) * (sib - me), j // 2, slot).start()
-
-    gram_steps(total_steps - RING, total_steps, to_b)
+    start_quarters(1, 4, True)
     gram_finish()
     lax.fori_loop(0, steps, wait_u, 0)
-    phase_b(None)
-    phase_c()
-    lax.fori_loop(0, steps, wait_r, 0)
+    for k in range(steps // 4):
+        some = range(4 * k, 4 * k + 4)
+        for c in some:
+            if c > 0:
+                load(diag, c, c).wait()
+            r_copy(DIAG, c, diag, sib).wait_recv()
+        total = grad[...]
+        for c in some:
+            total = total + dot(r_all[diag, :, cols(c)], xbuf[c])
+        grad[...] = total
+        for c in some:
+            load(a_order[c % 4], c // 4, c).start()
+    lax.fori_loop(0, steps, wait_relay, 0)
     local_passes()
 
     def sweep(t, carry):
         phase_a("b")
-        phase_b(GAMMA)
+        lax.fori_loop(0, steps, wait_r, 0)
+        phase_b()
+        lax.fori_loop(0, steps, wait_u, 0)
         phase_c()
-        lax.fori_loop(0, steps, wait_u, 0)
-        lax.fori_loop(0, steps, wait_r, 0)
+        lax.fori_loop(0, steps, wait_relay, 0)
         local_passes()
         return carry
 
     lax.fori_loop(0, SWEEPS - 1, sweep, 0)
 
     phase_a(None)
+    lax.fori_loop(0, steps, wait_r, 0)
+
+    def out_cols(q, c):
+        return pl.ds(pl.multiple_of(q * quarter + c * CHUNK, CHUNK), CHUNK)
 
     def o_copy(rel, c, q, target, source):
         return pltpu.make_async_remote_copy(
-            source, r_hbm.at[q, :, cols(c)], o_send.at[rel, c], o_recv.at[rel, c], **device(target))
+            source, r_hbm.at[:, out_cols(q, c)], o_send.at[rel, c], o_recv.at[rel, c], **device(target))
 
     def o_keep(c):
-        return pltpu.make_async_copy(r_own.at[:, cols(c)], r_hbm.at[me, :, cols(c)], o_local.at[c])
+        return pltpu.make_async_copy(r_own.at[:, cols(c)], r_hbm.at[:, out_cols(me, c)], o_local.at[c])
 
     def finish(c, carry):
         residual(c, GAMMA)
@@ -284,7 +336,7 @@
 
     def relay(c, carry):
         o_copy(CROSS, c, cross, cross, r_own.at[:, cols(c)]).wait_recv()
-        o_copy(DIAG, c, cross, sib, r_hbm.at[cross, :, cols(c)]).start()
+        o_copy(DIAG, c, cross, sib, r_hbm.at[:, out_cols(cross, c)]).start()
         return carry
 
     def drain(c, carry):
@@ -292,7 +344,7 @@
         o_copy(DIAG, c, diag, sib, r_own.at[:, cols(c)]).wait_recv()
         for rel, target in ((CROSS, cross), (SIB, sib)):
             o_copy(rel, c, me, target, r_own.at[:, cols(c)]).wait_send()
-        o_copy(DIAG, c, cross, sib, r_hbm.at[cross, :, cols(c)]).wait_send()
+        o_copy(DIAG, c, cross, sib, r_hbm.at[:, out_cols(cross, c)]).wait_send()
         o_keep(c).wait()
         return carry
 
@@ -311,44 +363,40 @@
         quarter = samples // group
         steps = quarter // CHUNK
         blocks = features // BLOCK
-        pad = ((0, ROWS - labels), (0, 0))
-        own = lax.dynamic_slice_in_dim(targets, lax.axis_index('feat') * quarter, quarter, 0)
-        w_t = jnp.pad(w_init.T, pad)
-        y_t = jnp.pad(own.T, pad)
         vmem = pl.BlockSpec(memory_space=pltpu.VMEM)
         anywhere = pl.BlockSpec(memory_space=pl.ANY)
         dma = pltpu.SemaphoreType.DMA
         weights, residual = pl.pallas_call(
             functools.partial(kernel, samples, group),
-            out_shape=(jax.ShapeDtypeStruct((ROWS, features), F32),
-                       jax.ShapeDtypeStruct((group, ROWS, quarter), F32)),
-            in_specs=[anywhere, vmem, vmem],
+            out_shape=(jax.ShapeDtypeStruct((labels, features), F32),
+                       jax.ShapeDtypeStruct((labels, samples), F32)),
+            in_specs=[anywhere, anywhere, anywhere],
             out_specs=(vmem, anywhere),
             scratch_shapes=[
                 pltpu.VMEM((RING, CHUNK, features), BF16),
+                pltpu.VMEM((features, CHUNK), BF16),
                 pltpu.VMEM((features, CHUNK), BF16),
                 pltpu.VMEM((blocks * (blocks + 1) // 2, BLOCK, BLOCK), F32),
                 pltpu.VMEM((features, features), BF16),
                 pltpu.VMEM((features, features), BF16),
                 pltpu.VMEM((1, features), F32),
-                pltpu.VMEM((ROWS, features), BF16),
-                pltpu.VMEM((ROWS, features), F32),
-                pltpu.VMEM((ROWS, quarter), F32),
-                pltpu.VMEM((group, ROWS, quarter), BF16),
-                pltpu.VMEM((ROWS, quarter), BF16),
-                pltpu.VMEM((3, ROWS, quarter), BF16),
-                pltpu.VMEM((3, ROWS, quarter), BF16),
+                pltpu.VMEM((labels, features), BF16),
+                pltpu.VMEM((labels, features), F32),
+                pltpu.VMEM((labels, quarter), F32),
+                pltpu.VMEM((group, labels, quarter), BF16),
+                pltpu.VMEM((labels, quarter), BF16),
+                pltpu.VMEM((3, labels, quarter), BF16),
+                pltpu.VMEM((3, labels, quarter), BF16),
                 dma((RING,)),
                 dma((3, steps)), dma((3, steps)),
                 dma((3, steps)), dma((3, steps)),
                 dma((3, steps)), dma((3, steps)),
-                dma((steps,)),
+                dma((steps,)), dma((2,)),
             ],
             compiler_params=pltpu.CompilerParams(
                 collective_id=0, has_side_effects=True, vmem_limit_bytes=67000000),
-        )(design, w_t, y_t)
-        residual = residual.transpose(0, 2, 1).reshape(samples, ROWS)[:, :labels]
-        return weights.T[:, :labels], residual
+        )(design, w_init.T, targets.T)
+        return weights.T, residual.T
 
     return jax.shard_map(
         per_device,

time: 555 us -> 529 us (0.953)
  Pallas kernels: 541 us -> 520 us
    pallas_call x1, Pallas kernels: 541 us -> 520 us  [per_device(): pl.pallas_call(functools.partial(kernel, samples, group), out_shape=(jax....]
    unnamed x3 -> x2, local copies, waits for them, and re-layouts: 0.91 us -> 8.43 us
    reshape x1 -> x0, local copies, waits for them, and re-layouts: 6.69 us -> none  [per_device(): residual = residual.transpose(0, 2, 1).reshape(samples, ROWS)[:, :labels]]
where the time goes in v2:
time: 529 us
  Pallas kernels  520 us (98%)
  local copies, waits for them, and re-layouts  8.43 us (2%)
    pallas_call x1, Pallas kernels, per_device(): pl.pallas_call(functools.partial(kernel, samples, group), out_shape=(jax....  520 us

profile of v2, /device:TPU:0, one launch (start us, length us, event | category | flops | bytes accessed | tf_op | source)
XLA Modules:
  0.0 529.0 jit_solution(2597668107097291352)
XLA Ops:
  0.6 519.9 %shard_map.50 = (f32[101,2048]{1,0:T(8,128)}, f32[101,16384]{1,0:T(8,128)}) custom-call(bf16[16384,2048]{1,0:T(8,128)(2,1)} %x_hbm.1, f32[101,2048]{1,0:T(8,128)} %bitcast.7, f32[101,16384]{1,0:T(8,128)} %bitcast.5), custom_call_target="tpu_custom_call" | custom-call | tf_op jit(solution)/shard_map/pallas_call | solution.py:369
  520.6 2.1 copy.7
  522.7 6.3 %copy.8 = f32[16384,101]{0,1:T(8,128)} copy(f32[16384,101]{0,1:T(8,128)} %bitcast.4) | data formatting | bytes 13238272

commit v3 on v2

--- a/solution.py
+++ b/solution.py
@@ -26,8 +26,34 @@
     return lax.dot_general(a, b, (dims, ((), ())), preferred_element_type=F32)
 
 
+MAIN = 96
+LANES = 128
+PACKED = 4 * MAIN + 24
+
+
+def pack(ref, value, tail_ref):
+    tail_ref[0:value.shape[0] - MAIN, :] = value[MAIN:]
+    for g in range(4):
+        ref[g * MAIN:(g + 1) * MAIN, :] = value[:MAIN, g * LANES:(g + 1) * LANES].astype(BF16)
+    part = [tail_ref[:, g * LANES:(g + 1) * LANES] for g in range(4)]
+    row = lax.broadcasted_iota(jnp.int32, part[0].shape, 0)
+    first = jnp.where(row < 5, part[0], pltpu.roll(part[3], 5, 0))
+    second = jnp.where(row < 5, part[1], pltpu.roll(part[3], 2, 0))
+    ref[4 * MAIN:PACKED, :] = jnp.concatenate([first, second, part[2]], axis=0).astype(BF16)
+
+
+def unpack(ref):
+    main = jnp.concatenate([ref[g * MAIN:(g + 1) * MAIN, :] for g in range(4)], axis=1)
+    rest = ref[4 * MAIN:PACKED, :].astype(F32)
+    part = [rest[8 * g:8 * (g + 1)] for g in range(3)]
+    row = lax.broadcasted_iota(jnp.int32, part[0].shape, 0)
+    last = jnp.where(row < 3, pltpu.roll(part[0], 3, 0), pltpu.roll(part[1], 6, 0))
+    tail = jnp.concatenate(part + [last], axis=1)
+    return main, tail
+
+
 def kernel(samples, group, x_hbm, w0_hbm, y_hbm, w_ref, r_hbm,
-           xbuf, xt0, xt1, gram, gram_hi, gram_lo, eta_ref, coef, grad, r_own, r_all, u_mine, u_out, u_in,
+           xbuf, xt0, xt1, gram, gram_hi, gram_lo, eta_ref, coef, grad, r_own, r_all, u_mine, u_out, u_in, tail_ref,
            x_sem, u_send, u_recv, r_send, r_recv, o_send, o_recv, o_local, in_sem):
     prob, me = lax.axis_index("prob"), lax.axis_index("feat")
     odd, half = lax.rem(me, 2), me // 2
@@ -106,23 +132,23 @@
 
     def u_copy(rel, c):
         return pltpu.make_async_remote_copy(
-            u_out.at[rel, :, cols(c)], u_in.at[rel, :, cols(c)],
+            u_out.at[rel, c], u_in.at[rel, c],
             u_send.at[rel, c], u_recv.at[rel, c], **device(partner[rel]))
 
     def r_copy(rel, c, q, target):
         return pltpu.make_async_remote_copy(
-            r_all.at[q, :, cols(c)], r_all.at[q, :, cols(c)],
+            r_all.at[q, c], r_all.at[q, c],
             r_send.at[rel, c], r_recv.at[rel, c], **device(target))
 
     a_rel = (CROSS, DIAG, SIB, None)
 
     def phase_a(nxt, together=1):
         def body(c, i, q, x):
-            u = dot(coef[...], x[...], ((1,), (1,))).astype(BF16)
+            u = dot(coef[...], x[...], ((1,), (1,)))
             if a_rel[i] is None:
-                u_mine[:, cols(c)] = u
+                u_mine[:, cols(c)] = u.astype(BF16)
                 return None
-            u_out[a_rel[i], :, cols(c)] = u
+            pack(u_out.at[a_rel[i], c], u, tail_ref)
             return u_copy(a_rel[i], c)
         rounds("a", nxt, body, together)
 
@@ -131,18 +157,24 @@
             u_copy(rel, c).wait_recv()
         total = u_mine[:, cols(c)].astype(F32)
         for rel in (SIB, CROSS, DIAG):
-            total = total + u_in[rel, :, cols(c)].astype(F32)
+            main, tail = unpack(u_in.at[rel, c])
+            both = jnp.concatenate([main.astype(F32), tail], axis=0)
+            total = total + both[:total.shape[0]]
         new = r_own[:, cols(c)] - factor * total
         r_own[:, cols(c)] = new
         return new
 
     def update(c, factor):
-        r_all[me, :, cols(c)] = residual(c, factor).astype(BF16)
+        pack(r_all.at[me, c], residual(c, factor), tail_ref)
         r_copy(CROSS, c, me, cross).start()
         r_copy(SIB, c, me, sib).start()
 
+    def residual_lhs(q, c):
+        main, tail = unpack(r_all.at[q, c])
+        return jnp.concatenate([main.astype(F32), tail], axis=0).astype(BF16)
+
     def accumulate(c, q, x):
-        grad[...] += dot(r_all[q, :, cols(c)], x[...])
+        grad[...] += dot(residual_lhs(q, c), x[...])[:grad.shape[0]]
 
     def phase_b():
         def body(c, i, q, x):
@@ -252,28 +284,28 @@
                 scaled = block * 0.25
                 rows, columns = slice(i * BLOCK, (i + 1) * BLOCK), slice(j * BLOCK, (j + 1) * BLOCK)
                 high = scaled.astype(BF16)
+                low = (scaled - high.astype(F32)).astype(BF16)
                 gram_hi[rows, columns] = high
-                gram_lo[rows, columns] = (scaled - high.astype(F32)).astype(BF16)
+                gram_lo[rows, columns] = low
                 if i != j:
-                    scaled = scaled.T
-                    high = scaled.astype(BF16)
-                    gram_hi[columns, rows] = high
-                    gram_lo[columns, rows] = (scaled - high.astype(F32)).astype(BF16)
+                    gram_hi[columns, rows] = high.T
+                    gram_lo[columns, rows] = low.T
         eta_ref[...] = jnp.broadcast_to(samples / (group * trace), eta_ref.shape)
 
     in_w = pltpu.make_async_copy(w0_hbm, w_ref, in_sem.at[0])
     in_y = pltpu.make_async_copy(
         y_hbm.at[:, pl.ds(pl.multiple_of(me * quarter, quarter), quarter)], r_own, in_sem.at[1])
     in_w.start()
+    tail_ref[...] = jnp.zeros_like(tail_ref)
     for k in range(RING):
         load(a_order[k % 4], k // 4, k).start()
     in_y.start()
+    gram[...] = jnp.zeros_like(gram)
+    grad[...] = jnp.zeros_like(grad)
     in_w.wait()
     coef[...] = w_ref[...].astype(BF16)
     pl.semaphore_wait(barrier, 3)
-    phase_a("start", 2)
-    gram[...] = jnp.zeros_like(gram)
-    grad[...] = jnp.zeros_like(grad)
+    phase_a("start", 4)
     in_y.wait()
 
     def first_update(c, carry):
@@ -295,7 +327,7 @@
             r_copy(DIAG, c, diag, sib).wait_recv()
         total = grad[...]
         for c in some:
-            total = total + dot(r_all[diag, :, cols(c)], xbuf[c])
+            total = total + dot(residual_lhs(diag, c), xbuf[c])[:total.shape[0]]
         grad[...] = total
         for c in some:
             load(a_order[c % 4], c // 4, c).start()
@@ -352,6 +384,30 @@
     lax.fori_loop(0, steps, relay, 0)
     lax.fori_loop(0, steps, wait_u, 0)
     lax.fori_loop(0, steps, drain, 0)
+
+
+def hand_over(w_in, r_in, w_out, r_out, w_buf, r_buf, in_sem, out_sem):
+    pieces = r_buf.shape[0]
+    width = r_buf.shape[2]
+
+    def views(k):
+        if k == pieces:
+            return w_in, w_buf, w_out
+        columns = pl.ds(k * width, width)
+        return r_in.at[:, columns], r_buf.at[k], r_out.at[:, columns]
+
+    ins, outs = [], []
+    for k in range(pieces + 1):
+        source, buffer, target = views(k)
+        ins.append(pltpu.make_async_copy(source, buffer, in_sem.at[k]))
+        outs.append(pltpu.make_async_copy(buffer, target, out_sem.at[k]))
+    for copy in ins:
+        copy.start()
+    for first, second in zip(ins, outs):
+        first.wait()
+        second.start()
+    for copy in outs:
+        copy.wait()
 
 
 def solution(mesh):
@@ -383,10 +439,11 @@
                 pltpu.VMEM((labels, features), BF16),
                 pltpu.VMEM((labels, features), F32),
                 pltpu.VMEM((labels, quarter), F32),
-                pltpu.VMEM((group, labels, quarter), BF16),
+                pltpu.VMEM((group, steps, PACKED, LANES), BF16),
                 pltpu.VMEM((labels, quarter), BF16),
-                pltpu.VMEM((3, labels, quarter), BF16),
-                pltpu.VMEM((3, labels, quarter), BF16),
+                pltpu.VMEM((3, steps, PACKED, LANES), BF16),
+                pltpu.VMEM((3, steps, PACKED, LANES), BF16),
+                pltpu.VMEM((8, CHUNK), F32),
                 dma((RING,)),
                 dma((3, steps)), dma((3, steps)),
                 dma((3, steps)), dma((3, steps)),
@@ -396,6 +453,19 @@
             compiler_params=pltpu.CompilerParams(
                 collective_id=0, has_side_effects=True, vmem_limit_bytes=67000000),
         )(design, w_init.T, targets.T)
+        pieces = 8
+        weights, residual = pl.pallas_call(
+            hand_over,
+            out_shape=(jax.ShapeDtypeStruct(weights.shape, F32), jax.ShapeDtypeStruct(residual.shape, F32)),
+            in_specs=[anywhere, anywhere],
+            out_specs=(anywhere, anywhere),
+            scratch_shapes=[
+                pltpu.VMEM(weights.shape, F32),
+                pltpu.VMEM((pieces, labels, samples // pieces), F32),
+                dma((pieces + 1,)), dma((pieces + 1,)),
+            ],
+            compiler_params=pltpu.CompilerParams(vmem_limit_bytes=66000000),
+        )(weights, residual)
         return weights.T, residual.T
 
     return jax.shard_map(

time: 529 us -> 522 us (0.987)
  local copies, waits for them, and re-layouts: 8.43 us -> 0 us
    unnamed x2 -> x0, local copies, waits for them, and re-layouts: 8.43 us -> none
    pallas_call x0 -> x1, Pallas kernels: none -> 6.08 us  [per_device(): pl.pallas_call(hand_over, out_shape=(jax.ShapeDtypeStruct(weights.shape,...]
where the time goes in v3:
time: 522 us
  Pallas kernels  521 us (100%)
    pallas_call x1, Pallas kernels, per_device(): pl.pallas_call(functools.partial(kernel, samples, group), out_shape=(jax....  515 us

profile of v3, /device:TPU:0, one launch (start us, length us, event | category | flops | bytes accessed | tf_op | source)
XLA Modules:
  0.0 521.8 jit_solution(5690980351621619616)
XLA Ops:
  0.6 514.9 %shard_map.50 = (f32[101,2048]{1,0:T(8,128)}, f32[101,16384]{1,0:T(8,128)}) custom-call(bf16[16384,2048]{1,0:T(8,128)(2,1)} %x_hbm.1, f32[101,2048]{1,0:T(8,128)} %bitcast.5, f32[101,16384]{1,0:T(8,128)} %bitcast.4), custom_call_target="tpu_custom_call" | custom-call | tf_op jit(solution)/shard_map/pallas_call | solution.py:425
  515.5 6.1 %shard_map.51 = (f32[101,2048]{1,0:T(8,128)}, f32[101,16384]{1,0:T(8,128)}) custom-call(f32[101,2048]{1,0:T(8,128)} %get-tuple-element.6.w_in, f32[101,16384]{1,0:T(8,128)} %get-tuple-element.7.r_in), custom_call_target="tpu_custom_call" | custom-call | tf_op jit(solution)/shard_map/pallas_call | solution.py:457

commit v4 on v3

--- a/solution.py
+++ b/solution.py
@@ -262,8 +262,9 @@
                 c = 2 * k + i
                 later[...] = xbuf[lax.rem(c + 1, RING)].T
                 gram_add(now, xbuf.at[c])
-                if with_gradient:
-                    accumulate(c, q, xbuf.at[c])
+            if with_gradient:
+                both = sum(dot(residual_lhs(q, 2 * k + i), xbuf[2 * k + i]) for i in range(2))
+                grad[...] += both[:grad.shape[0]]
             for i in range(2):
                 load(start_order(s + 1), 2 * k + i, 2 * k + i).start()
             return carry
@@ -453,7 +454,7 @@
             compiler_params=pltpu.CompilerParams(
                 collective_id=0, has_side_effects=True, vmem_limit_bytes=67000000),
         )(design, w_init.T, targets.T)
-        pieces = 8
+        pieces = 16
         weights, residual = pl.pallas_call(
             hand_over,
             out_shape=(jax.ShapeDtypeStruct(weights.shape, F32), jax.ShapeDtypeStruct(residual.shape, F32)),

time: 522 us -> 522 us (level)
  no operation moved by 1% of the time
where the time goes in v4:
time: 522 us
  Pallas kernels  521 us (100%)
    pallas_call x1, Pallas kernels, per_device(): pl.pallas_call(functools.partial(kernel, samples, group), out_shape=(jax....  515 us

profile of v4, /device:TPU:0, one launch (start us, length us, event | category | flops | bytes accessed | tf_op | source)
XLA Modules:
  0.0 522.1 jit_solution(14443460302880672720)
XLA Ops:
  0.6 515.0 %shard_map.50 = (f32[101,2048]{1,0:T(8,128)}, f32[101,16384]{1,0:T(8,128)}) custom-call(bf16[16384,2048]{1,0:T(8,128)(2,1)} %x_hbm.1, f32[101,2048]{1,0:T(8,128)} %bitcast.5, f32[101,16384]{1,0:T(8,128)} %bitcast.4), custom_call_target="tpu_custom_call" | custom-call | tf_op jit(solution)/shard_map/pallas_call | solution.py:426
  515.6 6.2 %shard_map.51 = (f32[101,2048]{1,0:T(8,128)}, f32[101,16384]{1,0:T(8,128)}) custom-call(f32[101,2048]{1,0:T(8,128)} %get-tuple-element.6.w_in, f32[101,16384]{1,0:T(8,128)} %get-tuple-element.7.r_in), custom_call_target="tpu_custom_call" | custom-call | tf_op jit(solution)/shard_map/pallas_call | solution.py:458
